TPU v7x, 32 devices: a whole 2x2x4 slice. The times are simulated.
32 devices in a mesh: depth: 8 (over z, x), tile: 4 (over y, core).
Axes of the slice: x: 2, y: 2, z: 4, core: 2. Of those that a mesh axis runs over, the one named last changes fastest.
Arguments:
- volume: bfloat16 [64, 256, 4096], P('depth', 'tile'), may hold values from -6 to 6
- shear: int32 [64], replicated, may hold values from -64 to 64, as said below
- footprint: int32 [8, 2], P('depth'), may hold values from 0 to 4096, as said below
Outputs:
- frame: float32 [4, 256, 4096], P(None, 'tile', 'depth')
Inputs may be any that keep to these rules, and one draw needn't show every extreme that they name: Offsets follow a linear tilt over the slices with small jitter; shear[0] and shear[63] are the two ends of the range, in either order. footprint[b, 0] < 1024 and footprint[b, 1] > 3072 for every brick.
All inputs are finite; a program needn't handle non-finite values.
Results may differ from a plain program's by a relative error of at most 0.00085.
Values may be sent and summed in bfloat16 or wider, within the bound.
No kernel may reach another device: no remote copies, remote signals or barrier semaphores. Data moves between devices by JAX's collectives and lax.ppermute only.
A program may use at most 64 MiB of HBM per device.

v0:
```python
import jax
import jax.numpy as jnp
from jax import lax
from jax.sharding import PartitionSpec as P

NY = 4096
SMAX = 64


def extended_2(x, sides, width):
    for axis, dim in sides:
        count, length = (lax.axis_size(axis), x.shape[dim])
        up = [(i, (i + 1) % count) for i in range(count - 1)]
        down = [(j, i) for i, j in up]
        last = lax.slice_in_dim(x, length - width, length, axis=dim)
        leading = lax.slice_in_dim(x, 0, width, axis=dim)
        before = lax.ppermute(last, axis, up)
        after = lax.ppermute(leading, axis, down)
        x = jnp.concatenate([before, x, after], axis=dim)
    return x


def colour(cur, gx, gy, gz, offset, low, high, absorb):
    norm = jnp.sqrt(gx * gx + gy * gy + gz * gz + 1.0)
    shade = 0.3 + 0.7 * jnp.abs(0.48 * gx + 0.6 * gy + 0.64 * gz) / norm
    alpha = 1.0 - jnp.exp(-absorb * cur * cur)
    rgba = jnp.stack(
        [
            shade * jax.nn.sigmoid(1.2 * cur + 0.2) * alpha,
            shade * jax.nn.sigmoid(-0.8 * cur) * alpha,
            shade * jax.nn.sigmoid(0.5 * cur - 0.3) * alpha,
            alpha,
        ]
    )
    padded = jnp.pad(rgba, ((0, 0), (0, 0), (SMAX, SMAX)))
    moved = lax.dynamic_slice_in_dim(padded, SMAX - offset, NY, 2)
    column = jnp.arange(NY, dtype=jnp.int32)
    inside = ((column >= low) & (column < high)).astype(jnp.float32)
    return moved * inside


def shards(volume, shear, footprint):
    slices = volume.shape[0]
    rows = volume.shape[1]
    bricks = lax.axis_size("depth")
    total = slices * bricks
    absorb = 2.0 / total
    flip = shear[0] > shear[total - 1]
    me = lax.axis_index("depth")
    local_shear = lax.dynamic_slice_in_dim(shear, me * slices, slices, 0)
    extended = extended_2(volume, (("depth", 0), ("tile", 1)), 1)

    def slice_step(step, acc):
        local = jnp.where(flip, slices - 1 - step, step).astype(jnp.int32)
        block = lax.dynamic_slice_in_dim(extended, local, 3, 0).astype(jnp.float32)
        cur = block[1, 1:-1]
        gz = 0.5 * (block[2, 1:-1] - block[0, 1:-1])
        gx = 0.5 * (block[1, 2:] - block[1, :-2])
        cols = jnp.pad(cur, ((0, 0), (1, 1)))
        gy = 0.5 * (cols[:, 2:] - cols[:, :-2])
        placed = colour(
            cur, gx, gy, gz, local_shear[local], footprint[0, 0], footprint[0, 1], absorb
        )
        return acc + (1.0 - acc[3:4]) * placed

    acc = lax.fori_loop(0, slices, slice_step, jnp.zeros((4, rows, NY), jnp.float32))
    partial_value = acc.astype(jnp.bfloat16)
    pieces = lax.all_to_all(partial_value[None], "depth", split_axis=3, concat_axis=0, tiled=True)

    def brick_step(position, image):
        source = jnp.where(flip, bricks - 1 - position, position).astype(jnp.int32)
        piece = lax.dynamic_index_in_dim(pieces, source, 0, keepdims=False).astype(jnp.float32)
        return image + (1.0 - image[3:4]) * piece

    start = jnp.zeros(pieces.shape[1:], jnp.float32)
    return lax.fori_loop(0, bricks, brick_step, start)


def solution(mesh):
    placed = (P("depth", "tile", None), P(), P("depth", None))
    return jax.shard_map(
        shards, mesh=mesh, in_specs=placed, out_specs=P(None, "tile", "depth"), check_vma=False
    )
```

profile of v0, /device:TPU:1, one launch (start us, length us, event | category | flops | bytes accessed | tf_op | source)
XLA Modules:
  0.0 268.8 jit_solution(5925467425739162417)
XLA Ops:
  1.3 4.0 %collective-permute-start = (bf16[1,64,4096]{2,1,0:T(8,128)(2,1)S(1)}, bf16[1,64,4096]{2,1,0:T(8,128)(2,1)S(1)}, u32[]{:S(2)}, u32[]{:S(2)}) collective-permute-start(bf16[1,64,4096]{2,1,0:T(8,128)(2,1)S(1)} %get-tuple-element.320), channel_id=1, source_target_pairs={{0,4},{4,8},{8,12},{12,16},{16,20},{20,24},{24,28},{1,5},{5,9},{9,... | collective-permute-start | bytes 1572872 | tf_op jit(solution)/shard_map/ppermute | solution.py:17
  7.3 19.7 %collective-permute-done = bf16[1,64,4096]{2,1,0:T(8,128)(2,1)S(1)} collective-permute-done((bf16[1,64,4096]{2,1,0:T(8,128)(2,1)S(1)}, bf16[1,64,4096]{2,1,0:T(8,128)(2,1)S(1)}, u32[]{:S(2)}, u32[]{:S(2)}) %collective-permute-start) | collective-permute-done | bytes 524320 | tf_op jit(solution)/shard_map/ppermute | solution.py:17
  27.1 2.5 constant_dynamic-update-slice_fusion.1
  30.0 4.6 %collective-permute-start.2 = (bf16[10,1,4096]{2,1,0:T(2,128)(2,1)S(1)}, bf16[10,1,4096]{2,1,0:T(2,128)(2,1)S(1)}, u32[]{:S(2)}, u32[]{:S(2)}) collective-permute-start(bf16[10,1,4096]{2,1,0:T(2,128)(2,1)S(1)} %get-tuple-element.317), channel_id=1, source_target_pairs={{0,1},{1,2},{2,3},{4,5},{5,6},{6,7},{8,9},{9,10},{10,11},{12,13},{... | collective-permute-start | bytes 245768 | tf_op jit(solution)/shard_map/ppermute | solution.py:17
  34.5 1.9 collective-permute-start.3
  38.3 2.9 %collective-permute-done.3 = bf16[10,1,4096]{2,1,0:T(2,128)(2,1)S(1)} collective-permute-done((bf16[10,1,4096]{2,1,0:T(2,128)(2,1)S(1)}, bf16[10,1,4096]{2,1,0:T(2,128)(2,1)S(1)}, u32[]{:S(2)}, u32[]{:S(2)}) %collective-permute-start.3) | collective-permute-done | bytes 81952 | tf_op jit(solution)/shard_map/ppermute | solution.py:18
  41.2 6.1 %pad_maximum_fusion = bf16[10,66,4096]{2,1,0:T(8,128)(2,1)} fusion(bf16[10,1,4096]{2,1,0:T(2,128)(2,1)S(1)} %collective-permute-done.3, bf16[10,64,4096]{2,1,0:T(8,128)(2,1)S(1)} %constant_dynamic-update-slice_fusion, bf16[10,1,4096]{2,1,0:T(2,128)(2,1)S(1)} %collective-permute-done.2), kind=kLoop, calls=%fused_computation.53 | loop fusion | flops 16220160 | bytes 10813440 | tf_op jit(solution)/shard_map/concatenate | solution.py:19
  47.3 135.7 %while.30 = (s32[]{:T(128)}, f32[4,64,4096]{2,1,0:T(8,128)}, pred[]{:T(512)}, bf16[10,66,4096]{2,1,0:T(8,128)(2,1)}, s32[8]{0:T(128)S(1)}, /*index=5*/s32[1,2]{1...) while((s32[]{:T(128)}, f32[4,64,4096]{2,1,0:T(8,128)}, ...), condition=%wide.region_1.2_spmd.clone, body=%wide.region_0.1_spmd.clone.sunk | while | flops 30973964 | bytes 48940876 | solution.py:66
  47.3 1.9 dynamic-slice_convert_fusion.2
  49.4 2.5 multiply_bitcast_fusion.5
  57.0 3.9 %fusion.44 = f32[4,64,4096]{2,1,0:T(8,128)} fusion(s32[]{:T(128)S(6)} %select_n.74, f32[1,64,4096]{2,1,0:T(8,128)S(1)} %get-tuple-element.391, f32[1,64,4096]{2,1,0:T(8,128)S(1)} %get-tuple-element.392, f32[1,64,4096]{2,1,0:T(8,128)S(1)} %copy-done, f32[1,64,4096]{2,1,0:T(8,128)S(1)} %get-tuple-element.394, f32[4096]{0:T(1024)S(1)} %fusion.42, ...), kind=kLoop, calls=%fused_computation.10.clone.1 | loop fusion | flops 15728640 | bytes 13649408 | tf_op jit(solution)/shard_map/while/body/eval_jaxpr/add | solution.py:64
  60.9 1.9 dynamic-slice_convert_fusion.2
  63.1 2.5 multiply_bitcast_fusion.5
  68.2 2.6 broadcast_select_fusion.4
  72.9 5.4 %fusion.44 = f32[4,64,4096]{2,1,0:T(8,128)} fusion(s32[]{:T(128)S(6)} %select_n.74, f32[1,64,4096]{2,1,0:T(8,128)S(1)} %get-tuple-element.391, f32[1,64,4096]{2,1,0:T(8,128)S(1)} %get-tuple-element.392, f32[1,64,4096]{2,1,0:T(8,128)S(1)} %copy-done, f32[1,64,4096]{2,1,0:T(8,128)S(1)} %get-tuple-element.394, f32[4096]{0:T(1024)S(1)} %fusion.42, ...), kind=kLoop, calls=%fused_computation.10.clone.1 | loop fusion | flops 15728640 | bytes 13649408 | tf_op jit(solution)/shard_map/while/body/eval_jaxpr/add | solution.py:64
  78.3 1.9 dynamic-slice_convert_fusion.2
  80.5 2.5 multiply_bitcast_fusion.5
  85.7 2.6 broadcast_select_fusion.4
  90.3 5.4 %fusion.44 = f32[4,64,4096]{2,1,0:T(8,128)} fusion(s32[]{:T(128)S(6)} %select_n.74, f32[1,64,4096]{2,1,0:T(8,128)S(1)} %get-tuple-element.391, f32[1,64,4096]{2,1,0:T(8,128)S(1)} %get-tuple-element.392, f32[1,64,4096]{2,1,0:T(8,128)S(1)} %copy-done, f32[1,64,4096]{2,1,0:T(8,128)S(1)} %get-tuple-element.394, f32[4096]{0:T(1024)S(1)} %fusion.42, ...), kind=kLoop, calls=%fused_computation.10.clone.1 | loop fusion | flops 15728640 | bytes 13649408 | tf_op jit(solution)/shard_map/while/body/eval_jaxpr/add | solution.py:64
  95.8 1.9 dynamic-slice_convert_fusion.2
  97.9 2.5 multiply_bitcast_fusion.5
  103.1 2.6 broadcast_select_fusion.4
  107.8 5.4 %fusion.44 = f32[4,64,4096]{2,1,0:T(8,128)} fusion(s32[]{:T(128)S(6)} %select_n.74, f32[1,64,4096]{2,1,0:T(8,128)S(1)} %get-tuple-element.391, f32[1,64,4096]{2,1,0:T(8,128)S(1)} %get-tuple-element.392, f32[1,64,4096]{2,1,0:T(8,128)S(1)} %copy-done, f32[1,64,4096]{2,1,0:T(8,128)S(1)} %get-tuple-element.394, f32[4096]{0:T(1024)S(1)} %fusion.42, ...), kind=kLoop, calls=%fused_computation.10.clone.1 | loop fusion | flops 15728640 | bytes 13649408 | tf_op jit(solution)/shard_map/while/body/eval_jaxpr/add | solution.py:64
  113.2 1.9 dynamic-slice_convert_fusion.2
  115.4 2.5 multiply_bitcast_fusion.5
  120.6 2.6 broadcast_select_fusion.4
  125.2 5.4 %fusion.44 = f32[4,64,4096]{2,1,0:T(8,128)} fusion(s32[]{:T(128)S(6)} %select_n.74, f32[1,64,4096]{2,1,0:T(8,128)S(1)} %get-tuple-element.391, f32[1,64,4096]{2,1,0:T(8,128)S(1)} %get-tuple-element.392, f32[1,64,4096]{2,1,0:T(8,128)S(1)} %copy-done, f32[1,64,4096]{2,1,0:T(8,128)S(1)} %get-tuple-element.394, f32[4096]{0:T(1024)S(1)} %fusion.42, ...), kind=kLoop, calls=%fused_computation.10.clone.1 | loop fusion | flops 15728640 | bytes 13649408 | tf_op jit(solution)/shard_map/while/body/eval_jaxpr/add | solution.py:64
  130.7 1.9 dynamic-slice_convert_fusion.2
  132.8 2.5 multiply_bitcast_fusion.5
  138.0 2.6 broadcast_select_fusion.4
  142.7 5.4 %fusion.44 = f32[4,64,4096]{2,1,0:T(8,128)} fusion(s32[]{:T(128)S(6)} %select_n.74, f32[1,64,4096]{2,1,0:T(8,128)S(1)} %get-tuple-element.391, f32[1,64,4096]{2,1,0:T(8,128)S(1)} %get-tuple-element.392, f32[1,64,4096]{2,1,0:T(8,128)S(1)} %copy-done, f32[1,64,4096]{2,1,0:T(8,128)S(1)} %get-tuple-element.394, f32[4096]{0:T(1024)S(1)} %fusion.42, ...), kind=kLoop, calls=%fused_computation.10.clone.1 | loop fusion | flops 15728640 | bytes 13649408 | tf_op jit(solution)/shard_map/while/body/eval_jaxpr/add | solution.py:64
  148.1 1.9 dynamic-slice_convert_fusion.2
  150.3 2.5 multiply_bitcast_fusion.5
  155.5 2.6 broadcast_select_fusion.4
  160.1 5.4 %fusion.44 = f32[4,64,4096]{2,1,0:T(8,128)} fusion(s32[]{:T(128)S(6)} %select_n.74, f32[1,64,4096]{2,1,0:T(8,128)S(1)} %get-tuple-element.391, f32[1,64,4096]{2,1,0:T(8,128)S(1)} %get-tuple-element.392, f32[1,64,4096]{2,1,0:T(8,128)S(1)} %copy-done, f32[1,64,4096]{2,1,0:T(8,128)S(1)} %get-tuple-element.394, f32[4096]{0:T(1024)S(1)} %fusion.42, ...), kind=kLoop, calls=%fused_computation.10.clone.1 | loop fusion | flops 15728640 | bytes 13649408 | tf_op jit(solution)/shard_map/while/body/eval_jaxpr/add | solution.py:64
  165.6 1.9 dynamic-slice_convert_fusion.2
  167.7 2.5 multiply_bitcast_fusion.5
  172.9 2.6 broadcast_select_fusion.4
  177.6 5.4 %fusion.44 = f32[4,64,4096]{2,1,0:T(8,128)} fusion(s32[]{:T(128)S(6)} %select_n.74, f32[1,64,4096]{2,1,0:T(8,128)S(1)} %get-tuple-element.391, f32[1,64,4096]{2,1,0:T(8,128)S(1)} %get-tuple-element.392, f32[1,64,4096]{2,1,0:T(8,128)S(1)} %copy-done, f32[1,64,4096]{2,1,0:T(8,128)S(1)} %get-tuple-element.394, f32[4096]{0:T(1024)S(1)} %fusion.42, ...), kind=kLoop, calls=%fused_computation.10.clone.1 | loop fusion | flops 15728640 | bytes 13649408 | tf_op jit(solution)/shard_map/while/body/eval_jaxpr/add | solution.py:64
  183.0 2.5 convert_element_type.52
  185.5 4.7 %copy.10 = bf16[4,64,4096]{1,0,2:T(4,128)(2,1)} copy(bf16[4,64,4096]{2,1,0:T(8,128)(2,1)S(1)} %convert_element_type.52) | data formatting | bytes 4194304
  190.2 5.3 %bitcast_bitcast_fusion = bf16[4096,1,4,64]{3,2,1,0:T(4,128)(2,1)} fusion(bf16[4,64,4096]{1,0,2:T(4,128)(2,1)} %copy.10), kind=kLoop, calls=%fused_computation.61 | loop fusion | bytes 4194304
  195.5 7.6 %reshape.29 = bf16[8,2,65536]{2,1,0:T(2,128)(2,1)} reshape(bf16[4096,1,4,64]{3,2,1,0:T(4,128)(2,1)} %bitcast_bitcast_fusion) | data formatting | bytes 4194304
  203.1 5.5 %all-to-all-start = ((bf16[8,2,65536]{2,1,0:T(2,128)(2,1)}), bf16[8,2,65536]{2,1,0:T(2,128)(2,1)S(1)}, u32[]{:S(2)}, u32[]{:S(2)}) async-start(bf16[8,2,65536]{2,1,0:T(2,128)(2,1)} %reshape.29), calls=%async_computation | async-start | bytes 4194304 | tf_op jit(solution)/shard_map/all_to_all | solution.py:68
  208.6 46.3 %all-to-all-done = bf16[8,2,65536]{2,1,0:T(2,128)(2,1)S(1)} async-done(((bf16[8,2,65536]{2,1,0:T(2,128)(2,1)}), bf16[8,2,65536]{2,1,0:T(2,128)(2,1)S(1)}, u32[]{:S(2)}, u32[]{:S(2)}) %all-to-all-start) | async-done | bytes 2097184 | tf_op jit(solution)/shard_map/all_to_all | solution.py:68
  254.9 5.0 %reshape.30 = bf16[4096,1,4,64]{3,2,1,0:T(4,128)(2,1)} reshape(bf16[8,2,65536]{2,1,0:T(2,128)(2,1)S(1)} %all-to-all-done) | data formatting | bytes 4194304
  259.9 5.6 %copy.9 = bf16[1,4,64,8,512]{4,2,1,3,0:T(8,128)(2,1)S(1)} copy(bf16[1,4,64,8,512]{2,1,4,3,0:T(4,128)(2,1)} %bitcast.87) | data formatting | bytes 4194304 | tf_op jit(solution)/shard_map/all_to_all | solution.py:68
  265.5 2.5 while.31
  (106 shorter events, 37.1 us)
Async XLA Ops:
  1.3 25.8 %collective-permute-start = (bf16[1,64,4096]{2,1,0:T(8,128)(2,1)S(1)}, bf16[1,64,4096]{2,1,0:T(8,128)(2,1)S(1)}, u32[]{:S(2)}, u32[]{:S(2)}) collective-permute-start(bf16[1,64,4096]{2,1,0:T(8,128)(2,1)S(1)} %get-tuple-element.320), channel_id=1, source_target_pairs={{0,4},{4,8},{8,12},{12,16},{16,20},{20,24},{24,28},{1,5},{5,9},{9,... | collective-permute-start | bytes 1572872 | tf_op jit(solution)/shard_map/ppermute | solution.py:17
  5.2 24.3 %collective-permute-start.1 = (bf16[1,64,4096]{2,1,0:T(8,128)(2,1)S(1)}, bf16[1,64,4096]{2,1,0:T(8,128)(2,1)S(1)}, u32[]{:S(2)}, u32[]{:S(2)}) collective-permute-start(bf16[1,64,4096]{2,1,0:T(8,128)(2,1)S(1)} %get-tuple-element.319), channel_id=1, source_target_pairs={{4,0},{8,4},{12,8},{16,12},{20,16},{24,20},{28,24},{5,1},{9,5},{13... | collective-permute-start | bytes 1572872 | tf_op jit(solution)/shard_map/ppermute | solution.py:18
  27.1 9.4 %copy-start.3 = (s32[64]{0:T(128)S(1)}, s32[64]{0:T(128)}, u32[]{:S(2)}) copy-start(s32[64]{0:T(128)} %param.8) | copy-start | bytes 772
  30.0 8.3 %collective-permute-start.2 = (bf16[10,1,4096]{2,1,0:T(2,128)(2,1)S(1)}, bf16[10,1,4096]{2,1,0:T(2,128)(2,1)S(1)}, u32[]{:S(2)}, u32[]{:S(2)}) collective-permute-start(bf16[10,1,4096]{2,1,0:T(2,128)(2,1)S(1)} %get-tuple-element.317), channel_id=1, source_target_pairs={{0,1},{1,2},{2,3},{4,5},{5,6},{6,7},{8,9},{9,10},{10,11},{12,13},{... | collective-permute-start | bytes 245768 | tf_op jit(solution)/shard_map/ppermute | solution.py:17
  34.5 6.6 %collective-permute-start.3 = (bf16[10,1,4096]{2,1,0:T(2,128)(2,1)S(1)}, bf16[10,1,4096]{2,1,0:T(2,128)(2,1)S(1)}, u32[]{:S(2)}, u32[]{:S(2)}) collective-permute-start(bf16[10,1,4096]{2,1,0:T(2,128)(2,1)S(1)} %get-tuple-element.318), channel_id=1, source_target_pairs={{1,0},{2,1},{3,2},{5,4},{6,5},{7,6},{9,8},{10,9},{11,10},{13,12},{... | collective-permute-start | bytes 245768 | tf_op jit(solution)/shard_map/ppermute | solution.py:18
  38.3 9.0 %copy-start.2 = (s32[1,2]{1,0:T(1,128)S(1)}, s32[1,2]{1,0:T(1,128)}, u32[]{:S(2)}) copy-start(s32[1,2]{1,0:T(1,128)} %param.9) | copy-start | bytes 28
  54.6 2.4 copy-start
  68.2 4.7 %copy-start = (f32[1,64,4096]{2,1,0:T(8,128)S(1)}, f32[1,64,4096]{2,1,0:T(8,128)}, u32[]{:S(2)}) copy-start(f32[1,64,4096]{2,1,0:T(8,128)} %get-tuple-element.393) | copy-start | bytes 3145732 | tf_op jit(solution)/shard_map/while
  85.7 4.7 %copy-start = (f32[1,64,4096]{2,1,0:T(8,128)S(1)}, f32[1,64,4096]{2,1,0:T(8,128)}, u32[]{:S(2)}) copy-start(f32[1,64,4096]{2,1,0:T(8,128)} %get-tuple-element.393) | copy-start | bytes 3145732 | tf_op jit(solution)/shard_map/while
  103.1 4.7 %copy-start = (f32[1,64,4096]{2,1,0:T(8,128)S(1)}, f32[1,64,4096]{2,1,0:T(8,128)}, u32[]{:S(2)}) copy-start(f32[1,64,4096]{2,1,0:T(8,128)} %get-tuple-element.393) | copy-start | bytes 3145732 | tf_op jit(solution)/shard_map/while
  120.6 4.7 %copy-start = (f32[1,64,4096]{2,1,0:T(8,128)S(1)}, f32[1,64,4096]{2,1,0:T(8,128)}, u32[]{:S(2)}) copy-start(f32[1,64,4096]{2,1,0:T(8,128)} %get-tuple-element.393) | copy-start | bytes 3145732 | tf_op jit(solution)/shard_map/while
  138.0 4.7 %copy-start = (f32[1,64,4096]{2,1,0:T(8,128)S(1)}, f32[1,64,4096]{2,1,0:T(8,128)}, u32[]{:S(2)}) copy-start(f32[1,64,4096]{2,1,0:T(8,128)} %get-tuple-element.393) | copy-start | bytes 3145732 | tf_op jit(solution)/shard_map/while
  155.4 4.7 %copy-start = (f32[1,64,4096]{2,1,0:T(8,128)S(1)}, f32[1,64,4096]{2,1,0:T(8,128)}, u32[]{:S(2)}) copy-start(f32[1,64,4096]{2,1,0:T(8,128)} %get-tuple-element.393) | copy-start | bytes 3145732 | tf_op jit(solution)/shard_map/while
  172.9 4.7 %copy-start = (f32[1,64,4096]{2,1,0:T(8,128)S(1)}, f32[1,64,4096]{2,1,0:T(8,128)}, u32[]{:S(2)}) copy-start(f32[1,64,4096]{2,1,0:T(8,128)} %get-tuple-element.393) | copy-start | bytes 3145732 | tf_op jit(solution)/shard_map/while
  203.1 51.8 %all-to-all-start = ((bf16[8,2,65536]{2,1,0:T(2,128)(2,1)}), bf16[8,2,65536]{2,1,0:T(2,128)(2,1)S(1)}, u32[]{:S(2)}, u32[]{:S(2)}) async-start(bf16[8,2,65536]{2,1,0:T(2,128)(2,1)} %reshape.29), calls=%async_computation | async-start | bytes 4194304 | tf_op jit(solution)/shard_map/all_to_all | solution.py:68
  268.0 0.8 copy-start.1
where the time goes:
time: 270 us; the launch traced here: 269 us
  other arithmetic  125 us (46%)
  waiting for transfers between devices  69 us (26%)
  local copies, waits for them, and re-layouts  44.4 us (16%)
  starting transfers between devices  17.2 us (6%)
  loops' own time  11.3 us (4%)
    all_to_all x1, waiting for transfers between devices, shards(): lax.all_to_all(partial_value[None], 'depth', split_axis=3, concat_axis=0,...  46.3 us
    add x8, other arithmetic, slice_step(): return acc + (1.0 - acc[3:4]) * placed  41.9 us
    another operation x16, other arithmetic, colour(): jnp.stack([shade * jax.nn.sigmoid(1.2 * cur + 0.2) * alpha, shade * jax.n...  26.2 us
    unnamed x12, local copies, waits for them, and re-layouts  25.9 us
    ppermute x2, waiting for transfers between devices, extended_2(): before = lax.ppermute(last, axis, up)  19.7 us
    while x16, other arithmetic  18.5 us
    convert_element_type x8, other arithmetic, slice_step(): block = lax.dynamic_slice_in_dim(extended, local, 3, 0).astype(jnp.float32)  15 us
    another operation x1, loops' own time, shards(): lax.fori_loop(0, slices, slice_step, jnp.zeros((4, rows, NY), jnp.float32))  11 us
  transfers between devices with their start and end apart: 5, of which 3 were waited for; matrix products, arithmetic and copies ran while one was open for 1% of the time, Pallas kernels for 0%

commit v1 on v0

v1 whole, which is shorter than its diff:
```python
import functools

import jax
import jax.numpy as jnp
from jax import lax
from jax.experimental import pallas as pl
from jax.experimental.pallas import tpu as pltpu
from jax.sharding import PartitionSpec as P

SMAX = 64
LANES = 128
ROWS = 16
LOG2E = 1.4426950408889634


def neighbours(x, axis, length):
    up = [(i, i + 1) for i in range(length - 1)]
    down = [(i + 1, i) for i in range(length - 1)]
    return up, down


def partial_kernel(
    absorb, low_high, shear, vol, prev, nxt, above, below, out, field, shades
):
    slices, rows, ny = vol.shape
    width = out.shape[3]
    low, high, flip = low_high[0], low_high[1], low_high[2]
    tiles = ny // LANES
    strips = rows // ROWS

    edge = jnp.zeros((slices + 2, rows + 16, LANES), jnp.float32)
    field[:, :, 0:LANES] = edge
    field[:, :, LANES + ny : 2 * LANES + ny] = edge
    shades[:, :, 0:LANES] = jnp.zeros((slices, ROWS, LANES), jnp.float32)
    shades[:, :, LANES + ny : 2 * LANES + ny] = jnp.zeros((slices, ROWS, LANES), jnp.float32)
    top = above[...].astype(jnp.float32)
    bottom = below[...].astype(jnp.float32)
    for s in range(slices):
        field[1 + s, 7:8, LANES : LANES + ny] = top[s : s + 1]
        field[1 + s, 8 + rows : 9 + rows, LANES : LANES + ny] = bottom[s : s + 1]

    def widen(strip, carry):
        r = pl.multiple_of(strip * ROWS, ROWS)
        source = pl.ds(r, ROWS)
        target = pl.ds(pl.multiple_of(r + 8, 8), ROWS)
        for s in range(slices):
            field[1 + s, target, LANES : LANES + ny] = vol[s, source, :].astype(jnp.float32)
        field[0, target, LANES : LANES + ny] = prev[source, :].astype(jnp.float32)
        field[slices + 1, target, LANES : LANES + ny] = nxt[source, :].astype(jnp.float32)
        return carry

    lax.fori_loop(0, strips, widen, 0)

    lane = lax.broadcasted_iota(jnp.int32, (ROWS, LANES), 1)
    span = 512

    def strip_step(strip, carry):
        r = pl.multiple_of(strip * ROWS, ROWS)

        def shade_step(i, carry):
            s = i // (ny // span)
            base = pl.multiple_of((i % (ny // span)) * span, span)
            here = pl.ds(pl.multiple_of(r + 8, 8), ROWS)
            wide = pl.ds(base, span + 2 * LANES)
            mid = pl.ds(pl.multiple_of(base + LANES, LANES), span)
            line = field[s + 1, here, wide]
            dy = line[:, LANES + 1 : LANES + 1 + span] - line[:, LANES - 1 : LANES - 1 + span]
            dz = field[s + 2, here, mid] - field[s, here, mid]
            tall = field[s + 1, pl.ds(r, ROWS + 16), mid]
            dx = tall[9 : 9 + ROWS] - tall[7 : 7 + ROWS]
            squares = dx * dx + dy * dy + dz * dz + 4.0
            along = (0.7 * 0.48) * dx + (0.7 * 0.6) * dy + (0.7 * 0.64) * dz
            shades[s, :, mid] = 0.15 + 0.5 * jnp.abs(along) * lax.rsqrt(squares)
            return carry

        lax.fori_loop(0, slices * (ny // span), shade_step, 0)

        def column_step(pair, carry):
            rate = []
            for j in range(2):
                column = lane + (2 * pair + j) * LANES
                inside = (column >= low) & (column < high)
                rate.append(jnp.where(inside, -absorb * LOG2E, 0.0))
            zero = jnp.zeros((ROWS, LANES), jnp.float32)
            clear = [zero + 1.0] * 2
            total = [zero] * 2
            colours = [[zero] * 3 for _ in range(2)]
            for step in range(slices):
                s = jnp.where(flip > 0, slices - 1 - step, step)
                shift = shear[s]
                turn = jnp.where(shift < 0, shift + LANES, shift)
                first = 2 * pair + jnp.where(shift < 0, 1, 0)
                moved = []
                for ref, index, height in ((field, s + 1, r + 8), (shades, s, 0)):
                    rolled = []
                    for j in range(3):
                        at = pl.ds(pl.multiple_of((first + j) * LANES, LANES), LANES)
                        if ref is field:
                            block = ref[index, pl.ds(pl.multiple_of(height, 8), ROWS), at]
                        else:
                            block = ref[index, :, at]
                        rolled.append(pltpu.roll(block, turn, 1))
                    moved.append(
                        [jnp.where(lane < turn, rolled[j], rolled[j + 1]) for j in range(2)]
                    )
                for j in range(2):
                    v, half_shade = moved[0][j], moved[1][j]
                    left = clear[j] * jnp.exp2(v * v * rate[j])
                    weight = (clear[j] - left) * half_shade
                    clear[j] = left
                    total[j] = total[j] + weight
                    arguments = (0.6 * v + 0.1, -0.4 * v, 0.25 * v - 0.15)
                    for c in range(3):
                        colours[j][c] = colours[j][c] + weight * jnp.tanh(arguments[c])
            for j in range(2):
                tile = 2 * pair + j
                per = width // LANES
                owner = tile // per
                at = pl.ds(pl.multiple_of((tile % per) * LANES, LANES), LANES)
                for c in range(3):
                    out[owner, c, pl.ds(r, ROWS), at] = (total[j] + colours[j][c]).astype(out.dtype)
                out[owner, 3, pl.ds(r, ROWS), at] = (1.0 - clear[j]).astype(out.dtype)
            return carry

        lax.fori_loop(0, tiles // 2, column_step, 0)
        return carry

    lax.fori_loop(0, strips, strip_step, 0)


def frame_kernel(flags, pieces, out):
    bricks = pieces.shape[0]
    rows = pieces.shape[2]

    def strip_step(strip, carry):
        at = pl.ds(pl.multiple_of(strip * ROWS, ROWS), ROWS)
        image = [jnp.zeros((ROWS, out.shape[2]), jnp.float32) for _ in range(4)]
        for position in range(bricks):
            source = jnp.where(flags[2] > 0, bricks - 1 - position, position)
            clear = 1.0 - image[3]
            image = [
                image[c] + clear * pieces[source, c, at, :].astype(jnp.float32) for c in range(4)
            ]
        for c in range(4):
            out[c, at, :] = image[c]
        return carry

    lax.fori_loop(0, rows // ROWS, strip_step, 0)


def shards(volume, shear, footprint):
    slices, rows, ny = volume.shape
    bricks = lax.axis_size("depth")
    tiles = lax.axis_size("tile")
    total = slices * bricks
    flip = (shear[0] > shear[total - 1]).astype(jnp.int32)
    me = lax.axis_index("depth")
    local_shear = lax.dynamic_slice_in_dim(shear, me * slices, slices, 0)
    flags = jnp.stack([footprint[0, 0], footprint[0, 1], flip])
    up, down = neighbours(volume, "depth", bricks)
    row_up, row_down = neighbours(volume, "tile", tiles)
    above = lax.ppermute(volume[:, rows - 1, :], "tile", row_up)
    below = lax.ppermute(volume[:, 0, :], "tile", row_down)
    prev = lax.ppermute(volume[slices - 1], "depth", up)
    nxt = lax.ppermute(volume[0], "depth", down)
    vmem = pl.BlockSpec(memory_space=pltpu.VMEM)
    smem = pl.BlockSpec(memory_space=pltpu.SMEM)
    width = ny // bricks
    partial_value = pl.pallas_call(
        functools.partial(partial_kernel, 2.0 / total),
        out_shape=jax.ShapeDtypeStruct((bricks, 4, rows, width), jnp.bfloat16),
        in_specs=[smem, smem] + [vmem] * 5,
        out_specs=vmem,
        scratch_shapes=[
            pltpu.VMEM((slices + 2, rows + 16, ny + 2 * LANES), jnp.float32),
            pltpu.VMEM((slices, ROWS, ny + 2 * LANES), jnp.float32),
        ],
        name="partial",
    )(flags, local_shear, volume, prev, nxt, above, below)
    pieces = lax.all_to_all(partial_value, "depth", split_axis=0, concat_axis=0, tiled=True)
    return pl.pallas_call(
        frame_kernel,
        out_shape=jax.ShapeDtypeStruct((4, rows, width), jnp.float32),
        in_specs=[smem, vmem],
        out_specs=vmem,
        name="frame",
    )(flags, pieces)


def solution(mesh):
    placed = (P("depth", "tile", None), P(), P("depth", None))
    return jax.shard_map(
        shards, mesh=mesh, in_specs=placed, out_specs=P(None, "tile", "depth"), check_vma=False
    )
```

time: 270 us -> 154 us (0.57)
  other arithmetic: 125 us -> 1.87 us
  Pallas kernels: 0 us -> 68.7 us
  waiting for transfers between devices: 69 us -> 6.65 us
  blocking collectives: 0 us -> 52.8 us
  local copies, waits for them, and re-layouts: 44.4 us -> 7.57 us
  loops' own time: 11.3 us -> 0 us
  starting transfers between devices: 17.2 us -> 12.3 us
    pallas_call x0 -> x2, Pallas kernels: none -> 68.7 us  [the longest x1 65.9 us: shards(): pl.pallas_call(functools.partial(partial_kernel, 2.0 / total), out_shape=...]
    all_to_all x0 -> x1, blocking collectives: none -> 52.8 us  [shards(): lax.all_to_all(partial_value, 'depth', split_axis=0, concat_axis=0, tiled...]
    all_to_all x1 -> x0, waiting for transfers between devices: 46.3 us -> none  [shards(): lax.all_to_all(partial_value[None], 'depth', split_axis=3, concat_axis=0,...]
    add x16 -> x0, other arithmetic: 43.6 us -> none  [the longest x8 41.9 us: slice_step(): return acc + (1.0 - acc[3:4]) * placed]
    convert_element_type x17 -> x0, other arithmetic: 28.1 us -> none  [the longest x8 15 us: slice_step(): block = lax.dynamic_slice_in_dim(extended, local, 3, 0).astype(jnp.float32)]
    unnamed x12 -> x10, local copies, waits for them, and re-layouts: 25.9 us -> 0.96 us
    another operation x16 -> x1, other arithmetic: 26.2 us -> 1.87 us  [shards(): flags = jnp.stack([footprint[0, 0], footprint[0, 1], flip])]
    while x16 -> x0, other arithmetic: 18.5 us -> none
  transfers between devices with their start and end apart: 5 -> 4, of which waited for: 3 -> 1; matrix products, arithmetic and copies ran while one was open for 1% -> 5% of each run, Pallas kernels for 0% -> 0%
where the time goes in v1:
time: 154 us; the launch traced here: 151 us
  Pallas kernels  68.7 us (45%)
  blocking collectives  52.8 us (34%)
  starting transfers between devices  12.3 us (8%)
  local copies, waits for them, and re-layouts  7.57 us (5%)
  waiting for transfers between devices  6.65 us (4%)
  other arithmetic  1.87 us (1%)
    pallas_call x1, Pallas kernels, shards(): pl.pallas_call(functools.partial(partial_kernel, 2.0 / total), out_shape=...  65.9 us
    all_to_all x1, blocking collectives, shards(): lax.all_to_all(partial_value, 'depth', split_axis=0, concat_axis=0, tiled...  52.8 us
    ppermute x1, waiting for transfers between devices, shards(): prev = lax.ppermute(volume[slices - 1], 'depth', up)  6.64 us
    ppermute x1, starting transfers between devices, shards(): prev = lax.ppermute(volume[slices - 1], 'depth', up)  4.59 us
    ppermute x1, starting transfers between devices, shards(): above = lax.ppermute(volume[:, rows - 1, :], 'tile', row_up)  4.51 us
  transfers between devices with their start and end apart: 4, of which 1 were waited for; matrix products, arithmetic and copies ran while one was open for 5% of the time, Pallas kernels for 0%

profile of v1, /device:TPU:1, one launch (start us, length us, event | category | flops | bytes accessed | tf_op | source)
XLA Modules:
  0.0 151.3 jit_solution(8217278714353900442)
XLA Ops:
  0.0 1.3 slice_bitcast_fusion
  1.3 1.3 collective-permute-start.1
  2.6 4.6 %collective-permute-start = (bf16[64,4096]{1,0:T(8,128)(2,1)S(1)}, bf16[64,4096]{1,0:T(8,128)(2,1)S(1)}, u32[]{:S(2)}, u32[]{:S(2)}) collective-permute-start(bf16[64,4096]{1,0:T(8,128)(2,1)S(1)} %get-tuple-element.8), channel_id=1, source_target_pairs={{0,4},{4,8},{8,12},{12,16},{16,20},{20,24},{24,28},{1,5},{5,9},{9,... | collective-permute-start | bytes 1572872 | tf_op jit(solution)/shard_map/ppermute | solution.py:164
  7.2 1.5 fusion
  8.6 0.1 copy.11
  8.7 4.5 %collective-permute-start.2 = (bf16[8,4096]{1,0:T(8,128)(2,1)S(1)}, bf16[8,4096]{1,0:T(8,128)(2,1)S(1)}, u32[]{:S(2)}, u32[]{:S(2)}) collective-permute-start(bf16[8,4096]{1,0:T(8,128)(2,1)S(1)} %bitcast.12), channel_id=1, source_target_pairs={{0,1},{1,2},{2,3},{4,5},{5,6},{6,7},{8,9},{9,10},{10,11},{12,13},{... | collective-permute-start | bytes 196616 | tf_op jit(solution)/shard_map/ppermute | solution.py:162
  13.2 0.1 copy.10
  13.3 1.9 %collective-permute-start.3 = (bf16[8,4096]{1,0:T(8,128)(2,1)S(1)}, bf16[8,4096]{1,0:T(8,128)(2,1)S(1)}, u32[]{:S(2)}, u32[]{:S(2)}) collective-permute-start(bf16[8,4096]{1,0:T(8,128)(2,1)S(1)} %bitcast.13), channel_id=1, source_target_pairs={{1,0},{2,1},{3,2},{5,4},{6,5},{7,6},{9,8},{10,9},{11,10},{13,12},{... | collective-permute-start | bytes 196616 | tf_op jit(solution)/shard_map/ppermute | solution.py:163
  15.3 1.2 dynamic_slice.3.shear
  16.5 1.3 fusion.2
  19.1 1.3 fusion.1
  20.4 1.9 %pad_add_fusion.low_high.flags = s32[3]{0:T(128)} fusion(s32[1]{0:T(128)S(6)} %convert_element_type.4, s32[1]{0:T(128)} %bitcast.1, s32[1]{0:T(128)} %bitcast), kind=kLoop, calls=%fused_computation.4 | loop fusion | flops 6 | bytes 24 | tf_op jit(solution)/shard_map/stack | solution.py:159
  22.3 0.0 collective-permute-done.2.above
  22.3 0.0 copy-start.2
  22.3 0.0 collective-permute-done.3.below
  22.3 0.0 copy-start.3
  22.3 0.0 collective-permute-done.1.nxt
  22.3 0.0 copy-start
  22.3 6.6 %collective-permute-done.prev = bf16[64,4096]{1,0:T(8,128)(2,1)S(1)} collective-permute-done((bf16[64,4096]{1,0:T(8,128)(2,1)S(1)}, bf16[64,4096]{1,0:T(8,128)(2,1)S(1)}, u32[]{:S(2)}, u32[]{:S(2)}) %collective-permute-start) | collective-permute-done | bytes 524320 | tf_op jit(solution)/shard_map/ppermute | solution.py:164
  29.0 0.0 copy-done.2
  29.0 0.0 copy-done.3
  29.0 0.0 copy-done
  29.0 0.0 copy-start.1
  29.0 0.8 copy-done.1
  29.8 65.9 %partial.1 = bf16[8,4,64,512]{3,2,1,0:T(8,128)(2,1)} custom-call(s32[3]{0:T(128)} %pad_add_fusion.low_high.flags, s32[8]{0:T(128)} %dynamic_slice.3.shear, bf16[8,64,4096]{2,1,0:T(8,128)(2,1)} %vol.1, bf16[64,4096]{1,0:T(8,128)(2,1)} %copy-done.1, bf16[64,4096]{1,0:T(8,128)(2,1)} %copy-done, bf16[8,4096]{1,0:T(8,128)(2,1)} %copy-done.2, ...), custom_call_target="tpu_custom_call" | custom-call | tf_op jit(solution)/shard_map/partial/pallas_call | solution.py:169
  95.7 52.8 %all_to_all.5.pieces = bf16[8,4,64,512]{3,2,1,0:T(8,128)(2,1)} all-to-all(bf16[8,4,64,512]{3,2,1,0:T(8,128)(2,1)} %partial.1), channel_id=1, replica_groups=mesh['depth'=8,'tile'=4] {'depth'}, dimensions={0} | all-to-all | bytes 4194304 | tf_op jit(solution)/shard_map/all_to_all | solution.py:180
  148.5 2.8 %frame.1 = f32[4,64,512]{2,1,0:T(8,128)} custom-call(s32[3]{0:T(128)} %pad_add_fusion.low_high.flags, bf16[8,4,64,512]{3,2,1,0:T(8,128)(2,1)} %all_to_all.5.pieces), custom_call_target="tpu_custom_call" | custom-call | tf_op jit(solution)/shard_map/frame/pallas_call | solution.py:181
Async XLA Ops:
  1.3 21.0 %collective-permute-start.1 = (bf16[64,4096]{1,0:T(8,128)(2,1)S(1)}, bf16[64,4096]{1,0:T(8,128)(2,1)S(1)}, u32[]{:S(2)}, u32[]{:S(2)}) collective-permute-start(bf16[64,4096]{1,0:T(8,128)(2,1)S(1)} %get-tuple-element.7), channel_id=1, source_target_pairs={{4,0},{8,4},{12,8},{16,12},{20,16},{24,20},{28,24},{5,1},{9,5},{13... | collective-permute-start | bytes 1572872 | tf_op jit(solution)/shard_map/ppermute | solution.py:165
  2.6 26.4 %collective-permute-start = (bf16[64,4096]{1,0:T(8,128)(2,1)S(1)}, bf16[64,4096]{1,0:T(8,128)(2,1)S(1)}, u32[]{:S(2)}, u32[]{:S(2)}) collective-permute-start(bf16[64,4096]{1,0:T(8,128)(2,1)S(1)} %get-tuple-element.8), channel_id=1, source_target_pairs={{0,4},{4,8},{8,12},{12,16},{16,20},{20,24},{24,28},{1,5},{5,9},{9,... | collective-permute-start | bytes 1572872 | tf_op jit(solution)/shard_map/ppermute | solution.py:164
  8.7 13.6 %collective-permute-start.2 = (bf16[8,4096]{1,0:T(8,128)(2,1)S(1)}, bf16[8,4096]{1,0:T(8,128)(2,1)S(1)}, u32[]{:S(2)}, u32[]{:S(2)}) collective-permute-start(bf16[8,4096]{1,0:T(8,128)(2,1)S(1)} %bitcast.12), channel_id=1, source_target_pairs={{0,1},{1,2},{2,3},{4,5},{5,6},{6,7},{8,9},{9,10},{10,11},{12,13},{... | collective-permute-start | bytes 196616 | tf_op jit(solution)/shard_map/ppermute | solution.py:162
  13.3 9.0 %collective-permute-start.3 = (bf16[8,4096]{1,0:T(8,128)(2,1)S(1)}, bf16[8,4096]{1,0:T(8,128)(2,1)S(1)}, u32[]{:S(2)}, u32[]{:S(2)}) collective-permute-start(bf16[8,4096]{1,0:T(8,128)(2,1)S(1)} %bitcast.13), channel_id=1, source_target_pairs={{1,0},{2,1},{3,2},{5,4},{6,5},{7,6},{9,8},{10,9},{11,10},{13,12},{... | collective-permute-start | bytes 196616 | tf_op jit(solution)/shard_map/ppermute | solution.py:163
  22.3 6.7 %copy-start.2 = (bf16[8,4096]{1,0:T(8,128)(2,1)}, bf16[8,4096]{1,0:T(8,128)(2,1)S(1)}, u32[]{:S(2)}) copy-start(bf16[8,4096]{1,0:T(8,128)(2,1)S(1)} %collective-permute-done.2.above) | copy-start | bytes 196612
  22.3 6.7 %copy-start.3 = (bf16[8,4096]{1,0:T(8,128)(2,1)}, bf16[8,4096]{1,0:T(8,128)(2,1)S(1)}, u32[]{:S(2)}) copy-start(bf16[8,4096]{1,0:T(8,128)(2,1)S(1)} %collective-permute-done.3.below) | copy-start | bytes 196612
  22.3 6.7 %copy-start = (bf16[64,4096]{1,0:T(8,128)(2,1)}, bf16[64,4096]{1,0:T(8,128)(2,1)S(1)}, u32[]{:S(2)}) copy-start(bf16[64,4096]{1,0:T(8,128)(2,1)S(1)} %collective-permute-done.1.nxt) | copy-start | bytes 1572868
  29.0 0.8 copy-start.1
